TPU v7x, 32 devices: a whole 2x2x4 slice. The times are simulated.
32 devices in a mesh: gz: 32 (over z, y, x, core).
Axes of the slice: x: 2, y: 2, z: 4, core: 2. Of those that a mesh axis runs over, the one named last changes fastest.
Arguments:
- coefficient: float32 [64, 512, 512], P('gz'), may hold values from 0.2 to 1.3
- initial_field: float32 [64, 512, 512], P('gz'), may hold values from -6 to 6
- observed: float32 [64, 512, 512], P('gz'), may hold values from -6 to 6
- misfit_weight: float32 [64, 512, 512], P('gz'), may hold values from 0.5 to 6, as said below
Outputs:
- coeff_gradient: float32 [64, 512, 512], P('gz')
- adjoint_field: float32 [64, 512, 512], P('gz')
- misfit: float32 [], replicated
Inputs may be any that keep to these rules, and one draw needn't show every extreme that they name: `misfit_weight`: positive cell weights.
All inputs are finite; a program needn't handle non-finite values.
Results may differ from a plain program's by a relative error of at most 0.00002.
Values sent between devices are 32-bit elements; how exact they have to be, the bound alone decides.
A program may use at most 128 MiB of HBM per device.

v0:
```python
import functools

import jax
import jax.numpy as jnp
from jax import lax
from jax.experimental import pallas as pl
from jax.experimental.pallas import tpu as pltpu
from jax.sharding import PartitionSpec as P

ITERS = 4
time_step = 0.125
MESH = pl.DeviceIdType.MESH
PAD = 8
TILE = 8
CHUNKS = 16


def kernel(n, rounds, cells, coef_hbm, init_hbm, obs_hbm, wgt_hbm, grad_out, adj_out, misfit_out,
           st, sl, halo, coef, obs, wgt, gacc, aacc, acc, part, edge_out, edge_in,
           in_send, in_recv, halo_send, halo_recv, edge_send, edge_recv,
           out_send, out_recv, psend_sem, precv_sem):
    own, ny, nx = coef_hbm.shape
    planes, half = 2 * own, ny // 2
    rows = half // CHUNKS
    exchanges = 2 * ITERS
    me = lax.axis_index("gz")
    q = me % 4
    base = me - q
    h, s = q // 2, q % 2
    lower, upper = me - 3 + 2 * s, me + 1 + 2 * s
    mate = me + 2 - 4 * h
    has_lo = lower >= 0
    has_hi = upper < n
    partners = []
    for r in range(rounds):
        bit = 1 << r
        partners.append(me + bit * (1 - 2 * ((me // bit) % 2)))

    barrier = pltpu.get_barrier_semaphore()

    def greet(device):
        pl.semaphore_signal(barrier, inc=1, device_id=(device,), device_id_type=MESH)

    for i in range(1, 4):
        greet(base + (q + i) % 4)
    for partner in partners[2:]:
        greet(partner)
    outside_lo = (s == 0) & has_lo
    outside_hi = (s == 1) & has_hi

    @pl.when(outside_lo)
    def _():
        greet(lower)

    @pl.when(outside_hi)
    def _():
        greet(upper)

    zero_rows = jnp.zeros((PAD, nx), jnp.float32)
    outer = pl.multiple_of(h * (PAD + half), PAD)
    inner = pl.multiple_of((1 - h) * (PAD + half), PAD)

    crossing = outside_lo | outside_hi

    @pl.when(crossing)
    def _():
        pl.semaphore_wait(barrier, rounds + 2)

    @pl.when(jnp.logical_not(crossing))
    def _():
        pl.semaphore_wait(barrier, rounds + 1)

    hbm = (init_hbm, coef_hbm, obs_hbm, wgt_hbm)
    held = (None, coef, obs, wgt)

    def place(side_half, j):
        return j if side_half == 1 else CHUNKS - 1 - j

    def feed(array, j):
        for to in range(2):
            dest = base + 2 * to + q // 2
            row = place(to, j) * rows
            slot = pl.ds(s * own, own)
            if array == 0:
                if isinstance(j, int) and j == 0:
                    start = row if to == 0 else half - PAD
                    src = init_hbm.at[:, pl.ds(start, rows + PAD), :]
                    dst = st.at[0, slot, pl.ds(PAD + row if to == 0 else 0, rows + PAD), :]
                else:
                    src = init_hbm.at[:, pl.ds(pl.multiple_of(to * half + row, PAD), rows), :]
                    dst = st.at[0, slot, pl.ds(pl.multiple_of(PAD + row, PAD), rows), :]
            else:
                src = hbm[array].at[:, pl.ds(pl.multiple_of(to * half + row, PAD), rows), :]
                dst = held[array].at[slot, pl.ds(pl.multiple_of(row, PAD), rows), :]
            arrived = in_recv.at[array, s, j]

            @pl.when(dest == me)
            def _():
                pltpu.make_async_copy(src, dst, arrived).start()

            @pl.when(dest != me)
            def _():
                pltpu.make_async_remote_copy(
                    src_ref=src, dst_ref=dst, send_sem=in_send.at[array, to], recv_sem=arrived,
                    device_id=(dest,), device_id_type=MESH,
                ).start()

    def await_copy(ref, sem):
        pltpu.make_async_copy(ref, ref, sem).wait()

    def fed(array, j, at):
        for slot in range(2):
            arrived = in_recv.at[array, slot, j]
            mine = pl.ds(slot * own, own)
            if array == 0:
                @pl.when(j == 0)
                def _():
                    start = pl.multiple_of((1 - h) * (PAD + at), PAD)
                    await_copy(st.at[0, mine, pl.ds(start, rows + PAD), :], arrived)

                @pl.when(j != 0)
                def _():
                    await_copy(st.at[0, mine, pl.ds(pl.multiple_of(PAD + at, PAD), rows), :], arrived)
            else:
                await_copy(held[array].at[mine, pl.ds(at, rows), :], arrived)

    for j in range(3):
        feed(0, j)
        feed(1, j)

    def clear_pad(e, carry):
        for p in range(planes):
            st[e, p, pl.ds(outer, PAD), :] = zero_rows
        return carry

    lax.fori_loop(0, exchanges, clear_pad, 0)

    def clear_halo(side):
        def clear(i, carry):
            e = i // (half // PAD)
            row = pl.multiple_of((i % (half // PAD)) * PAD, PAD)
            halo[side, e, pl.ds(row, PAD), :] = zero_rows
            return carry

        lax.fori_loop(0, exchanges * (half // PAD), clear, 0)

    @pl.when(jnp.logical_not(has_lo))
    def _():
        clear_halo(0)

    @pl.when(jnp.logical_not(has_hi))
    def _():
        clear_halo(1)

    acc[...] = jnp.zeros_like(acc)
    def send(e, at, j):
        here = pl.ds(at, rows)
        padded = pl.ds(pl.multiple_of(PAD + at, PAD), rows)

        def copy(side, device):
            pltpu.make_async_remote_copy(
                src_ref=st.at[e, (planes - 1) * (1 - side), padded, :],
                dst_ref=halo.at[side, e, here, :],
                send_sem=halo_send.at[side, e], recv_sem=halo_recv.at[side, e, j],
                device_id=(device,), device_id_type=MESH,
            ).start()

        @pl.when(has_hi)
        def _():
            copy(0, upper)

        @pl.when(has_lo)
        def _():
            copy(1, lower)

    def receive(e, at, j):
        here = pl.ds(at, rows)

        @pl.when(has_lo)
        def _():
            await_copy(halo.at[0, e, here, :], halo_recv.at[0, e, j])

        @pl.when(has_hi)
        def _():
            await_copy(halo.at[1, e, here, :], halo_recv.at[1, e, j])

    def edge_copy(e):
        return pltpu.make_async_remote_copy(
            src_ref=edge_out.at[e], dst_ref=edge_in.at[e],
            send_sem=edge_send.at[e], recv_sem=edge_recv.at[e],
            device_id=(mate,), device_id_type=MESH,
        )

    def stage_edge(e):
        at = pl.multiple_of(PAD + (1 - h) * (half - PAD), PAD)
        for p in range(planes):
            block = st[e, p, pl.ds(at, PAD), :]
            edge_out[e, p:p + 1, :] = jnp.where(h == 0, block[PAD - 1:PAD], block[0:1])

    def take_edge(e):
        edge_copy(e).wait_recv()
        for p in range(planes):
            st[e, p, pl.ds(inner, PAD), :] = jnp.broadcast_to(edge_in[e, p:p + 1, :], (PAD, nx))

    lane = lax.broadcasted_iota(jnp.int32, (TILE, nx), 1)
    leftmost = lane == 0
    rightmost = lane == nx - 1

    def laplace(e, p, row):
        here = pl.ds(row, TILE)
        padded = pl.ds(pl.multiple_of(row + PAD, PAD), TILE)
        tall = st[e, p, pl.ds(row, TILE + 2 * PAD), :]
        mid = tall[PAD:PAD + TILE]
        beside = tall[PAD + 1:PAD + 1 + TILE] + tall[PAD - 1:PAD - 1 + TILE]
        beside = beside + jnp.where(rightmost, 0.0, pltpu.roll(mid, nx - 1, 1))
        beside = beside + jnp.where(leftmost, 0.0, pltpu.roll(mid, 1, 1))
        above = st[e, p + 1, padded, :] if p + 1 < planes else halo[1, e, here, :]
        below = st[e, p - 1, padded, :] if p > 0 else halo[0, e, here, :]
        return mid, beside + above + below - 6.0 * mid

    def ship(which, source, target, m):
        at = pl.multiple_of((CHUNKS - 2 - 2 * m) * (1 - h) * rows + 2 * m * h * rows, PAD)
        for o in range(2):
            dest = base + 2 * s + o
            src = source.at[pl.ds(o * own, own), pl.ds(at, 2 * rows), :]
            dst = target.at[:, pl.ds(pl.multiple_of(h * half + at, PAD), 2 * rows), :]

            @pl.when(dest == me)
            def _():
                pltpu.make_async_copy(src, dst, out_recv.at[which, h]).start()

            @pl.when(dest != me)
            def _():
                pltpu.make_async_remote_copy(
                    src_ref=src, dst_ref=dst, send_sem=out_send.at[which, o],
                    recv_sem=out_recv.at[which, h], device_id=(dest,), device_id_type=MESH,
                ).start()

    def stage(e, j):
        at = pl.multiple_of((CHUNKS - 1 - j) * (1 - h) * rows + j * h * rows, PAD)
        if e == 0:
            fed(1, j, at)
        else:
            @pl.when(j == 0)
            def _():
                take_edge(e)
        if e == ITERS - 1:
            fed(2, j, at)
            fed(3, j, at)
        receive(e, at, j)

        def tile(t, carry):
            row = pl.multiple_of(at + t * TILE, TILE)
            here = pl.ds(row, TILE)
            padded = pl.ds(pl.multiple_of(row + PAD, PAD), TILE)
            for p in range(planes):
                mid, slope = laplace(e, p, row)
                if e < ITERS - 1:
                    sl[e, p, here, :] = slope
                    st[e + 1, p, padded, :] = mid + time_step * coef[p, here, :] * slope
                elif e == ITERS - 1:
                    c = coef[p, here, :]
                    resid = mid + time_step * c * slope - obs[p, here, :]
                    weighted = wgt[p, here, :] * resid
                    acc[...] += weighted * resid
                    aacc[p, here, :] = weighted
                    gacc[p, here, :] = time_step * weighted * slope
                    st[e + 1, p, padded, :] = c * weighted
                else:
                    lam = aacc[p, here, :] + time_step * slope
                    aacc[p, here, :] = lam
                    if e < exchanges - 1:
                        gacc[p, here, :] += time_step * lam * sl[exchanges - 2 - e, p, here, :]
                        st[e + 1, p, padded, :] = coef[p, here, :] * lam
            return carry

        lax.fori_loop(0, rows // TILE, tile, 0)
        if e < exchanges - 1:
            @pl.when(j == 0)
            def _():
                stage_edge(e + 1)

            send(e + 1, at, j)

            @pl.when(j == 0)
            def _():
                edge_copy(e + 1).start()

    def exchange(r):
        return pltpu.make_async_remote_copy(
            src_ref=part.at[2 * r], dst_ref=part.at[2 * r + 1],
            send_sem=psend_sem.at[r], recv_sem=precv_sem.at[r],
            device_id=(partners[r],), device_id_type=MESH,
        )

    def total_round(r):
        if r == 0:
            whole = acc[...]
            narrow = whole[:, 0:128]
            for i in range(1, nx // 128):
                narrow = narrow + whole[:, 128 * i:128 * i + 128]
            part[0] = narrow
        else:
            exchange(r - 1).wait_recv()
            part[2 * r] = part[2 * r - 2] + part[2 * r - 1]
        exchange(r).start()

    summed = CHUNKS + ITERS - 1
    ticks = CHUNKS + exchanges

    def tick(t, carry):
        @pl.when(t < CHUNKS)
        def _():
            at = pl.multiple_of((CHUNKS - 1 - t) * (1 - h) * rows + t * h * rows, PAD)
            fed(0, t, at)
            send(0, at, t)

        for e in range(exchanges):
            j = t - 1 - e

            @pl.when((j >= 0) & (j < CHUNKS))
            def _():
                stage(e, j)

        @pl.when(t + 3 < CHUNKS)
        def _():
            feed(0, t + 3)
            feed(1, t + 3)

        late = t + 2 - ITERS + 1

        @pl.when((late >= 0) & (late < CHUNKS))
        def _():
            feed(2, late)
            feed(3, late)

        for which, source, target, begin in ((0, gacc, grad_out, CHUNKS - 2), (1, aacc, adj_out, CHUNKS - 1)):
            m, final = t - begin, CHUNKS // 2 - 1

            @pl.when((m >= 0) & (m < final))
            def _():
                ship(which, source, target, m)

            @pl.when(m == final + 1)
            def _():
                ship(which, source, target, final)

        for r in range(min(rounds, ticks - summed)):
            @pl.when(t == summed + r)
            def _():
                total_round(r)

        return carry

    lax.fori_loop(0, ticks, tick, 0)
    for r in range(ticks - summed, rounds):
        total_round(r)

    exchange(rounds - 1).wait_recv()
    whole = part[2 * rounds - 2] + part[2 * rounds - 1]
    whole = jnp.sum(jnp.sum(whole, axis=1, keepdims=True), axis=0, keepdims=True)
    misfit_out[...] = jnp.sqrt(jnp.broadcast_to(whole, (8, 128)) / cells + 1e-06)

    for which, target in enumerate((grad_out, adj_out)):
        for side in range(2):
            await_copy(target.at[:, pl.ds(side * half, half), :], out_recv.at[which, side])
    for which, source in enumerate((gacc, aacc)):
        for o in range(2):
            @pl.when(base + 2 * s + o != me)
            def _():
                await_copy(source.at[pl.ds(o * own, own)], out_send.at[which, o])
    for array in range(4):
        for to in range(2):
            @pl.when(base + 2 * to + q // 2 != me)
            def _():
                extra = PAD if array == 0 else 0
                await_copy(hbm[array].at[:, pl.ds(0, half + extra), :], in_send.at[array, to])
    for e in range(exchanges):
        @pl.when(has_hi)
        def _():
            await_copy(halo.at[0, e], halo_send.at[0, e])

        @pl.when(has_lo)
        def _():
            await_copy(halo.at[1, e], halo_send.at[1, e])
    for e in range(1, exchanges):
        edge_copy(e).wait_send()
    for r in range(rounds):
        exchange(r).wait_send()


def solution(mesh):
    n = mesh.shape["gz"]
    rounds = n.bit_length() - 1

    def on_device(coefficient, initial_field, observed, misfit_weight):
        own, ny, nx = coefficient.shape
        planes, half = 2 * own, ny // 2
        slab = jax.ShapeDtypeStruct(coefficient.shape, jnp.float32)
        exchanges = 2 * ITERS
        block = pltpu.VMEM((planes, half, nx), jnp.float32)
        edge = pltpu.VMEM((exchanges, planes, nx), jnp.float32)
        dma = pltpu.SemaphoreType.DMA
        grad, adj, misfit = pl.pallas_call(
            functools.partial(kernel, n, rounds, float(n * own * ny * nx)),
            out_shape=(slab, slab, jax.ShapeDtypeStruct((8, 128), jnp.float32)),
            in_specs=[pl.BlockSpec(memory_space=pl.ANY)] * 4,
            out_specs=[pl.BlockSpec(memory_space=pl.ANY)] * 2 + [pl.BlockSpec(memory_space=pltpu.VMEM)],
            scratch_shapes=[
                pltpu.VMEM((exchanges, planes, half + 2 * PAD, nx), jnp.float32),
                pltpu.VMEM((ITERS - 1, planes, half, nx), jnp.float32),
                pltpu.VMEM((2, exchanges, half, nx), jnp.float32),
                block, block, block, block, block,
                pltpu.VMEM((TILE, nx), jnp.float32),
                pltpu.VMEM((2 * rounds, 8, 128), jnp.float32),
                edge, edge,
                dma((4, 2)), dma((4, 2, CHUNKS)),
                dma((2, exchanges)), dma((2, exchanges, CHUNKS)),
                dma((exchanges,)), dma((exchanges,)),
                dma((2, 2)), dma((2, 2)),
                dma((rounds,)), dma((rounds,)),
            ],
            compiler_params=pltpu.CompilerParams(
                collective_id=0, has_side_effects=True, vmem_limit_bytes=48 * 1024 * 1024
            ),
        )(coefficient, initial_field, observed, misfit_weight)
        scale = misfit[0, 0]
        return grad / scale, adj / scale, scale

    placed = P("gz", None, None)
    return jax.shard_map(
        on_device,
        mesh=mesh,
        in_specs=(placed,) * 4,
        out_specs=(placed, placed, P()),
        check_vma=False,
    )
```

profile of v0, /device:TPU:1, one launch (start us, length us, event | category | flops | bytes accessed | tf_op | source)
XLA Modules:
  0.0 150.7 jit_solution(10801964308971221192)
XLA Ops:
  0.6 146.4 %shard_map.67 = (f32[2,512,512]{2,1,0:T(8,128)S(1)}, f32[2,512,512]{2,1,0:T(8,128)S(1)}, f32[8,128]{1,0:T(8,128)S(1)}) custom-call(f32[2,512,512]{2,1,0:T(8,128)} %coef_hbm.1, f32[2,512,512]{2,1,0:T(8,128)} %init_hbm.1, f32[2,512,512]{2,1,0:T(8,128)} %obs_hbm.1, f32[2,512,512]{2,1,0:T(8,128)} %wgt_hbm.1), custom_call_target="tpu_custom_call" | custom-call | tf_op jit(solution)/shard_map/pallas_call | solution.py:404
  147.1 0.5 slice.3
  147.6 3.2 %broadcast_divide_fusion = (f32[2,512,512]{2,1,0:T(8,128)}, f32[2,512,512]{2,1,0:T(8,128)}) fusion(f32[2,512,512]{2,1,0:T(8,128)S(1)} %get-tuple-element.8, f32[]{:T(128)} %bitcast, f32[2,512,512]{2,1,0:T(8,128)S(1)} %get-tuple-element.6), kind=kLoop, calls=%fused_computation | loop fusion | flops 1048576 | bytes 8388612 | tf_op jit(solution)/shard_map/div | solution.py:428
where the time goes:
time: 152 us; the launch traced here: 151 us
  Pallas kernels  146 us (96%)
  other arithmetic  3.16 us (2%)
    pallas_call x1, Pallas kernels, on_device(): pl.pallas_call(functools.partial(kernel, n, rounds, float(n * own * ny *...  146 us
    div x1, other arithmetic, on_device(): return (grad / scale, adj / scale, scale)  3.16 us

commit v1 on v0

--- a/solution.py
+++ b/solution.py
@@ -35,6 +35,8 @@
     for r in range(rounds):
         bit = 1 << r
         partners.append(me + bit * (1 - 2 * ((me // bit) % 2)))
+    sums = [partners[0]] + partners[2:]
+    free = s == h
 
     barrier = pltpu.get_barrier_semaphore()
 
@@ -43,8 +45,6 @@
 
     for i in range(1, 4):
         greet(base + (q + i) % 4)
-    for partner in partners[2:]:
-        greet(partner)
     outside_lo = (s == 0) & has_lo
     outside_hi = (s == 1) & has_hi
 
@@ -64,11 +64,11 @@
 
     @pl.when(crossing)
     def _():
-        pl.semaphore_wait(barrier, rounds + 2)
+        pl.semaphore_wait(barrier, 4)
 
     @pl.when(jnp.logical_not(crossing))
     def _():
-        pl.semaphore_wait(barrier, rounds + 1)
+        pl.semaphore_wait(barrier, 3)
 
     hbm = (init_hbm, coef_hbm, obs_hbm, wgt_hbm)
     held = (None, coef, obs, wgt)
@@ -82,13 +82,8 @@
             row = place(to, j) * rows
             slot = pl.ds(s * own, own)
             if array == 0:
-                if isinstance(j, int) and j == 0:
-                    start = row if to == 0 else half - PAD
-                    src = init_hbm.at[:, pl.ds(start, rows + PAD), :]
-                    dst = st.at[0, slot, pl.ds(PAD + row if to == 0 else 0, rows + PAD), :]
-                else:
-                    src = init_hbm.at[:, pl.ds(pl.multiple_of(to * half + row, PAD), rows), :]
-                    dst = st.at[0, slot, pl.ds(pl.multiple_of(PAD + row, PAD), rows), :]
+                src = init_hbm.at[:, pl.ds(pl.multiple_of(to * half + row, PAD), rows), :]
+                dst = st.at[0, slot, pl.ds(pl.multiple_of(PAD + row, PAD), rows), :]
             else:
                 src = hbm[array].at[:, pl.ds(pl.multiple_of(to * half + row, PAD), rows), :]
                 dst = held[array].at[slot, pl.ds(pl.multiple_of(row, PAD), rows), :]
@@ -113,14 +108,7 @@
             arrived = in_recv.at[array, slot, j]
             mine = pl.ds(slot * own, own)
             if array == 0:
-                @pl.when(j == 0)
-                def _():
-                    start = pl.multiple_of((1 - h) * (PAD + at), PAD)
-                    await_copy(st.at[0, mine, pl.ds(start, rows + PAD), :], arrived)
-
-                @pl.when(j != 0)
-                def _():
-                    await_copy(st.at[0, mine, pl.ds(pl.multiple_of(PAD + at, PAD), rows), :], arrived)
+                await_copy(st.at[0, mine, pl.ds(pl.multiple_of(PAD + at, PAD), rows), :], arrived)
             else:
                 await_copy(held[array].at[mine, pl.ds(at, rows), :], arrived)
 
@@ -240,10 +228,11 @@
         at = pl.multiple_of((CHUNKS - 1 - j) * (1 - h) * rows + j * h * rows, PAD)
         if e == 0:
             fed(1, j, at)
-        else:
-            @pl.when(j == 0)
-            def _():
-                take_edge(e)
+
+        @pl.when(j == 0)
+        def _():
+            take_edge(e)
+
         if e == ITERS - 1:
             fed(2, j, at)
             fed(3, j, at)
@@ -290,7 +279,14 @@
         return pltpu.make_async_remote_copy(
             src_ref=part.at[2 * r], dst_ref=part.at[2 * r + 1],
             send_sem=psend_sem.at[r], recv_sem=precv_sem.at[r],
-            device_id=(partners[r],), device_id_type=MESH,
+            device_id=(sums[r],), device_id_type=MESH,
+        )
+
+    def across(o):
+        return pltpu.make_async_remote_copy(
+            src_ref=part.at[2 * rounds - 2], dst_ref=part.at[2 * rounds - 1],
+            send_sem=psend_sem.at[rounds - 1 + o], recv_sem=precv_sem.at[rounds - 1],
+            device_id=(base + 2 * (1 - h) + o,), device_id_type=MESH,
         )
 
     def total_round(r):
@@ -303,7 +299,13 @@
         else:
             exchange(r - 1).wait_recv()
             part[2 * r] = part[2 * r - 2] + part[2 * r - 1]
-        exchange(r).start()
+        if r < rounds - 1:
+            exchange(r).start()
+        else:
+            @pl.when(free)
+            def _():
+                across(0).start()
+                across(1).start()
 
     summed = CHUNKS + ITERS - 1
     ticks = CHUNKS + exchanges
@@ -313,6 +315,12 @@
         def _():
             at = pl.multiple_of((CHUNKS - 1 - t) * (1 - h) * rows + t * h * rows, PAD)
             fed(0, t, at)
+
+            @pl.when(t == 0)
+            def _():
+                stage_edge(0)
+                edge_copy(0).start()
+
             send(0, at, t)
 
         for e in range(exchanges):
@@ -356,7 +364,7 @@
     for r in range(ticks - summed, rounds):
         total_round(r)
 
-    exchange(rounds - 1).wait_recv()
+    across(0).wait_recv()
     whole = part[2 * rounds - 2] + part[2 * rounds - 1]
     whole = jnp.sum(jnp.sum(whole, axis=1, keepdims=True), axis=0, keepdims=True)
     misfit_out[...] = jnp.sqrt(jnp.broadcast_to(whole, (8, 128)) / cells + 1e-06)
@@ -373,8 +381,7 @@
         for to in range(2):
             @pl.when(base + 2 * to + q // 2 != me)
             def _():
-                extra = PAD if array == 0 else 0
-                await_copy(hbm[array].at[:, pl.ds(0, half + extra), :], in_send.at[array, to])
+                await_copy(hbm[array].at[:, pl.ds(0, half), :], in_send.at[array, to])
     for e in range(exchanges):
         @pl.when(has_hi)
         def _():
@@ -383,10 +390,15 @@
         @pl.when(has_lo)
         def _():
             await_copy(halo.at[1, e], halo_send.at[1, e])
-    for e in range(1, exchanges):
+    for e in range(exchanges):
         edge_copy(e).wait_send()
-    for r in range(rounds):
+    for r in range(rounds - 1):
         exchange(r).wait_send()
+
+    @pl.when(free)
+    def _():
+        across(0).wait_send()
+        across(1).wait_send()
 
 
 def solution(mesh):
@@ -418,7 +430,7 @@
                 dma((2, exchanges)), dma((2, exchanges, CHUNKS)),
                 dma((exchanges,)), dma((exchanges,)),
                 dma((2, 2)), dma((2, 2)),
-                dma((rounds,)), dma((rounds,)),
+                dma((rounds + 1,)), dma((rounds,)),
             ],
             compiler_params=pltpu.CompilerParams(
                 collective_id=0, has_side_effects=True, vmem_limit_bytes=48 * 1024 * 1024

time: 152 us -> 149 us (0.980)
  Pallas kernels: 146 us -> 144 us
    pallas_call x1, Pallas kernels: 146 us -> 144 us  [on_device(): pl.pallas_call(functools.partial(kernel, n, rounds, float(n * own * ny *...]
where the time goes in v1:
time: 149 us
  Pallas kernels  144 us (97%)
  other arithmetic  3.16 us (2%)
    pallas_call x1, Pallas kernels, on_device(): pl.pallas_call(functools.partial(kernel, n, rounds, float(n * own * ny *...  144 us
    div x1, other arithmetic, on_device(): return (grad / scale, adj / scale, scale)  3.16 us

profile of v1, /device:TPU:1, one launch (start us, length us, event | category | flops | bytes accessed | tf_op | source)
XLA Modules:
  0.0 148.8 jit_solution(2302149547396779848)
XLA Ops:
  0.6 144.5 %shard_map.67 = (f32[2,512,512]{2,1,0:T(8,128)S(1)}, f32[2,512,512]{2,1,0:T(8,128)S(1)}, f32[8,128]{1,0:T(8,128)S(1)}) custom-call(f32[2,512,512]{2,1,0:T(8,128)} %coef_hbm.1, f32[2,512,512]{2,1,0:T(8,128)} %init_hbm.1, f32[2,512,512]{2,1,0:T(8,128)} %obs_hbm.1, f32[2,512,512]{2,1,0:T(8,128)} %wgt_hbm.1), custom_call_target="tpu_custom_call" | custom-call | tf_op jit(solution)/shard_map/pallas_call | solution.py:416
  145.1 0.5 slice.3
  145.6 3.2 %broadcast_divide_fusion = (f32[2,512,512]{2,1,0:T(8,128)}, f32[2,512,512]{2,1,0:T(8,128)}) fusion(f32[2,512,512]{2,1,0:T(8,128)S(1)} %get-tuple-element.8, f32[]{:T(128)} %bitcast, f32[2,512,512]{2,1,0:T(8,128)S(1)} %get-tuple-element.6), kind=kLoop, calls=%fused_computation | loop fusion | flops 1048576 | bytes 8388612 | tf_op jit(solution)/shard_map/div | solution.py:440

commit v2 on v1

--- a/solution.py
+++ b/solution.py
@@ -13,12 +13,14 @@
 PAD = 8
 TILE = 8
 CHUNKS = 16
+RING = 4
+PIECE = 128
 
 
 def kernel(n, rounds, cells, coef_hbm, init_hbm, obs_hbm, wgt_hbm, grad_out, adj_out, misfit_out,
            st, sl, halo, coef, obs, wgt, gacc, aacc, acc, part, edge_out, edge_in,
            in_send, in_recv, halo_send, halo_recv, edge_send, edge_recv,
-           out_send, out_recv, psend_sem, precv_sem):
+           out_send, out_recv, psend_sem, precv_sem, first, first_sem):
     own, ny, nx = coef_hbm.shape
     planes, half = 2 * own, ny // 2
     rows = half // CHUNKS
@@ -38,6 +40,12 @@
     sums = [partners[0]] + partners[2:]
     free = s == h
 
+    hbm = (init_hbm, coef_hbm, obs_hbm, wgt_hbm)
+    held = (None, coef, obs, wgt)
+    for array in range(2):
+        src = hbm[array].at[:, pl.ds(pl.multiple_of(half - h * rows, PAD), rows), :]
+        pltpu.make_async_copy(src, first.at[array], first_sem).start()
+
     barrier = pltpu.get_barrier_semaphore()
 
     def greet(device):
@@ -69,9 +77,6 @@
     @pl.when(jnp.logical_not(crossing))
     def _():
         pl.semaphore_wait(barrier, 3)
-
-    hbm = (init_hbm, coef_hbm, obs_hbm, wgt_hbm)
-    held = (None, coef, obs, wgt)
 
     def place(side_half, j):
         return j if side_half == 1 else CHUNKS - 1 - j
@@ -87,31 +92,37 @@
             else:
                 src = hbm[array].at[:, pl.ds(pl.multiple_of(to * half + row, PAD), rows), :]
                 dst = held[array].at[slot, pl.ds(pl.multiple_of(row, PAD), rows), :]
-            arrived = in_recv.at[array, s, j]
+            arrived = in_recv.at[array // 2, j]
+            distant = dest != me
+            if isinstance(j, int) and j == 0:
+                across_chips = q // 2 != to
+                distant = distant & (q // 2 == to)
+
+                @pl.when(across_chips)
+                def _():
+                    pltpu.make_async_remote_copy(
+                        src_ref=first.at[array], dst_ref=dst, send_sem=in_send.at[to], recv_sem=arrived,
+                        device_id=(dest,), device_id_type=MESH,
+                    ).start()
 
             @pl.when(dest == me)
             def _():
                 pltpu.make_async_copy(src, dst, arrived).start()
 
-            @pl.when(dest != me)
+            @pl.when(distant)
             def _():
                 pltpu.make_async_remote_copy(
-                    src_ref=src, dst_ref=dst, send_sem=in_send.at[array, to], recv_sem=arrived,
+                    src_ref=src, dst_ref=dst, send_sem=in_send.at[to], recv_sem=arrived,
                     device_id=(dest,), device_id_type=MESH,
                 ).start()
 
     def await_copy(ref, sem):
         pltpu.make_async_copy(ref, ref, sem).wait()
 
-    def fed(array, j, at):
-        for slot in range(2):
-            arrived = in_recv.at[array, slot, j]
-            mine = pl.ds(slot * own, own)
-            if array == 0:
-                await_copy(st.at[0, mine, pl.ds(pl.multiple_of(PAD + at, PAD), rows), :], arrived)
-            else:
-                await_copy(held[array].at[mine, pl.ds(at, rows), :], arrived)
-
+    def fed(kind, j):
+        await_copy(st.at[pl.ds(0, 2), :, pl.ds(0, rows), :], in_recv.at[kind, j])
+
+    await_copy(first, first_sem)
     for j in range(3):
         feed(0, j)
         feed(1, j)
@@ -149,7 +160,7 @@
             pltpu.make_async_remote_copy(
                 src_ref=st.at[e, (planes - 1) * (1 - side), padded, :],
                 dst_ref=halo.at[side, e, here, :],
-                send_sem=halo_send.at[side, e], recv_sem=halo_recv.at[side, e, j],
+                send_sem=halo_send.at[side], recv_sem=halo_recv.at[e, j % RING],
                 device_id=(device,), device_id_type=MESH,
             ).start()
 
@@ -163,19 +174,20 @@
 
     def receive(e, at, j):
         here = pl.ds(at, rows)
-
-        @pl.when(has_lo)
-        def _():
-            await_copy(halo.at[0, e, here, :], halo_recv.at[0, e, j])
-
-        @pl.when(has_hi)
-        def _():
-            await_copy(halo.at[1, e, here, :], halo_recv.at[1, e, j])
+        arrived = halo_recv.at[e, j % RING]
+
+        @pl.when(has_lo & has_hi)
+        def _():
+            await_copy(halo.at[:, e, here, :], arrived)
+
+        @pl.when(jnp.logical_not(has_lo & has_hi))
+        def _():
+            await_copy(halo.at[0, e, here, :], arrived)
 
     def edge_copy(e):
         return pltpu.make_async_remote_copy(
             src_ref=edge_out.at[e], dst_ref=edge_in.at[e],
-            send_sem=edge_send.at[e], recv_sem=edge_recv.at[e],
+            send_sem=edge_send, recv_sem=edge_recv.at[e % 2],
             device_id=(mate,), device_id_type=MESH,
         )
 
@@ -215,27 +227,23 @@
 
             @pl.when(dest == me)
             def _():
-                pltpu.make_async_copy(src, dst, out_recv.at[which, h]).start()
+                pltpu.make_async_copy(src, dst, out_recv).start()
 
             @pl.when(dest != me)
             def _():
                 pltpu.make_async_remote_copy(
-                    src_ref=src, dst_ref=dst, send_sem=out_send.at[which, o],
-                    recv_sem=out_recv.at[which, h], device_id=(dest,), device_id_type=MESH,
+                    src_ref=src, dst_ref=dst, send_sem=out_send.at[o],
+                    recv_sem=out_recv, device_id=(dest,), device_id_type=MESH,
                 ).start()
 
     def stage(e, j):
         at = pl.multiple_of((CHUNKS - 1 - j) * (1 - h) * rows + j * h * rows, PAD)
-        if e == 0:
-            fed(1, j, at)
-
         @pl.when(j == 0)
         def _():
             take_edge(e)
 
         if e == ITERS - 1:
-            fed(2, j, at)
-            fed(3, j, at)
+            fed(1, j)
         receive(e, at, j)
 
         def tile(t, carry):
@@ -278,14 +286,14 @@
     def exchange(r):
         return pltpu.make_async_remote_copy(
             src_ref=part.at[2 * r], dst_ref=part.at[2 * r + 1],
-            send_sem=psend_sem.at[r], recv_sem=precv_sem.at[r],
+            send_sem=psend_sem, recv_sem=precv_sem.at[r],
             device_id=(sums[r],), device_id_type=MESH,
         )
 
     def across(o):
         return pltpu.make_async_remote_copy(
             src_ref=part.at[2 * rounds - 2], dst_ref=part.at[2 * rounds - 1],
-            send_sem=psend_sem.at[rounds - 1 + o], recv_sem=precv_sem.at[rounds - 1],
+            send_sem=psend_sem, recv_sem=precv_sem.at[rounds - 1],
             device_id=(base + 2 * (1 - h) + o,), device_id_type=MESH,
         )
 
@@ -314,7 +322,7 @@
         @pl.when(t < CHUNKS)
         def _():
             at = pl.multiple_of((CHUNKS - 1 - t) * (1 - h) * rows + t * h * rows, PAD)
-            fed(0, t, at)
+            fed(0, t)
 
             @pl.when(t == 0)
             def _():
@@ -369,36 +377,55 @@
     whole = jnp.sum(jnp.sum(whole, axis=1, keepdims=True), axis=0, keepdims=True)
     misfit_out[...] = jnp.sqrt(jnp.broadcast_to(whole, (8, 128)) / cells + 1e-06)
 
-    for which, target in enumerate((grad_out, adj_out)):
-        for side in range(2):
-            await_copy(target.at[:, pl.ds(side * half, half), :], out_recv.at[which, side])
-    for which, source in enumerate((gacc, aacc)):
-        for o in range(2):
-            @pl.when(base + 2 * s + o != me)
-            def _():
-                await_copy(source.at[pl.ds(o * own, own)], out_send.at[which, o])
-    for array in range(4):
-        for to in range(2):
-            @pl.when(base + 2 * to + q // 2 != me)
-            def _():
-                await_copy(hbm[array].at[:, pl.ds(0, half), :], in_send.at[array, to])
-    for e in range(exchanges):
-        @pl.when(has_hi)
-        def _():
-            await_copy(halo.at[0, e], halo_send.at[0, e])
-
-        @pl.when(has_lo)
-        def _():
-            await_copy(halo.at[1, e], halo_send.at[1, e])
-    for e in range(exchanges):
-        edge_copy(e).wait_send()
-    for r in range(rounds - 1):
-        exchange(r).wait_send()
+    slabs = st.at[pl.ds(0, 2), :, pl.ds(0, half), :]
+    await_copy(slabs, out_recv)
+    for o in range(2):
+        @pl.when(base + 2 * s + o != me)
+        def _():
+            await_copy(coef, out_send.at[o])
+    for to in range(2):
+        @pl.when(base + 2 * to + q // 2 != me)
+        def _():
+            await_copy(slabs, in_send.at[to])
+
+    @pl.when(has_hi)
+    def _():
+        await_copy(halo.at[0], halo_send.at[0])
+
+    @pl.when(has_lo)
+    def _():
+        await_copy(halo.at[1], halo_send.at[1])
+
+    await_copy(edge_out, edge_send)
 
     @pl.when(free)
     def _():
-        across(0).wait_send()
-        across(1).wait_send()
+        await_copy(part.at[pl.ds(0, rounds + 1)], psend_sem)
+
+    @pl.when(jnp.logical_not(free))
+    def _():
+        await_copy(part.at[pl.ds(0, rounds - 1)], psend_sem)
+
+
+def finish(grad, adj, misfit, grad_out, adj_out, misfit_out, scaled, sem):
+    own, ny, nx = grad.shape
+    scale = misfit[...]
+    misfit_out[...] = scale[0:1, 0:1]
+    inverse = 1.0 / scale
+    wide = jnp.concatenate([inverse] * (nx // 128), axis=1)
+    for which, (source, target) in enumerate(((grad, grad_out), (adj, adj_out))):
+        for p in range(own):
+            def piece(i, carry):
+                at = pl.multiple_of(i * PIECE, PIECE)
+                for r in range(PIECE // TILE):
+                    row = pl.multiple_of(at + r * TILE, TILE)
+                    scaled[which, p, pl.ds(row, TILE), :] = source[p, pl.ds(row, TILE), :] * wide
+                here = pl.ds(at, PIECE)
+                pltpu.make_async_copy(scaled.at[which, p, here, :], target.at[p, here, :], sem).start()
+                return carry
+
+            lax.fori_loop(0, ny // PIECE, piece, 0)
+    pltpu.make_async_copy(scaled, scaled, sem).wait()
 
 
 def solution(mesh):
@@ -426,18 +453,27 @@
                 pltpu.VMEM((TILE, nx), jnp.float32),
                 pltpu.VMEM((2 * rounds, 8, 128), jnp.float32),
                 edge, edge,
-                dma((4, 2)), dma((4, 2, CHUNKS)),
-                dma((2, exchanges)), dma((2, exchanges, CHUNKS)),
-                dma((exchanges,)), dma((exchanges,)),
-                dma((2, 2)), dma((2, 2)),
-                dma((rounds + 1,)), dma((rounds,)),
+                dma((2,)), dma((2, CHUNKS)),
+                dma((2,)), dma((exchanges, RING)),
+                dma, dma((2,)),
+                dma((2,)), dma,
+                dma, dma((rounds,)),
+                pltpu.VMEM((2, own, half // CHUNKS, nx), jnp.float32), dma,
             ],
             compiler_params=pltpu.CompilerParams(
                 collective_id=0, has_side_effects=True, vmem_limit_bytes=48 * 1024 * 1024
             ),
         )(coefficient, initial_field, observed, misfit_weight)
-        scale = misfit[0, 0]
-        return grad / scale, adj / scale, scale
+        vmem = pl.BlockSpec(memory_space=pltpu.VMEM)
+        grad, adj, misfit = pl.pallas_call(
+            finish,
+            out_shape=(slab, slab, jax.ShapeDtypeStruct((1, 1), jnp.float32)),
+            in_specs=[vmem] * 3,
+            out_specs=[pl.BlockSpec(memory_space=pltpu.HBM)] * 2 + [vmem],
+            scratch_shapes=[pltpu.VMEM((2, *coefficient.shape), jnp.float32), dma],
+            compiler_params=pltpu.CompilerParams(vmem_limit_bytes=6 * 1024 * 1024),
+        )(grad, adj, misfit)
+        return grad, adj, misfit.reshape(())
 
     placed = P("gz", None, None)
     return jax.shard_map(

time: 149 us -> 145 us (0.973)
  other arithmetic: 3.16 us -> 0 us
    div x1 -> x0, other arithmetic: 3.16 us -> none  [on_device(): return (grad / scale, adj / scale, scale)]
    pallas_call x1, Pallas kernels: 144 us -> 142 us  [on_device(): pl.pallas_call(functools.partial(kernel, n, rounds, float(n * own * ny *...]
    pallas_call x0 -> x1, Pallas kernels: none -> 2.55 us  [on_device(): pl.pallas_call(finish, out_shape=(slab, slab, jax.ShapeDtypeStruct((1, 1)...]
where the time goes in v2:
time: 145 us
  Pallas kernels  144 us (99%)
    pallas_call x1, Pallas kernels, on_device(): pl.pallas_call(functools.partial(kernel, n, rounds, float(n * own * ny *...  142 us

profile of v2, /device:TPU:1, one launch (start us, length us, event | category | flops | bytes accessed | tf_op | source)
XLA Modules:
  0.0 145.0 jit_solution(7862707285524195393)
XLA Ops:
  0.6 141.8 %shard_map.67 = (f32[2,512,512]{2,1,0:T(8,128)S(1)}, f32[2,512,512]{2,1,0:T(8,128)S(1)}, f32[8,128]{1,0:T(8,128)S(1)}) custom-call(f32[2,512,512]{2,1,0:T(8,128)} %coef_hbm.1, f32[2,512,512]{2,1,0:T(8,128)} %init_hbm.1, f32[2,512,512]{2,1,0:T(8,128)} %obs_hbm.1, f32[2,512,512]{2,1,0:T(8,128)} %wgt_hbm.1), custom_call_target="tpu_custom_call" | custom-call | tf_op jit(solution)/shard_map/pallas_call | solution.py:443
  142.4 2.5 %shard_map.68 = (f32[2,512,512]{2,1,0:T(8,128)}, f32[2,512,512]{2,1,0:T(8,128)}, f32[1,1]{1,0:T(1,128)}) custom-call(f32[2,512,512]{2,1,0:T(8,128)S(1)} %get-tuple-element.9.grad, f32[2,512,512]{2,1,0:T(8,128)S(1)} %get-tuple-element.10.adj, f32[8,128]{1,0:T(8,128)S(1)} %get-tuple-element.11.misfit), custom_call_target="tpu_custom_call" | custom-call | tf_op jit(solution)/shard_map/pallas_call | solution.py:468

commit v3 on v2

--- a/solution.py
+++ b/solution.py
@@ -15,6 +15,7 @@
 CHUNKS = 16
 RING = 4
 PIECE = 128
+SHIP = 12
 
 
 def kernel(n, rounds, cells, coef_hbm, init_hbm, obs_hbm, wgt_hbm, grad_out, adj_out, misfit_out,
@@ -51,32 +52,33 @@
     def greet(device):
         pl.semaphore_signal(barrier, inc=1, device_id=(device,), device_id_type=MESH)
 
-    for i in range(1, 4):
-        greet(base + (q + i) % 4)
-    outside_lo = (s == 0) & has_lo
-    outside_hi = (s == 1) & has_hi
-
-    @pl.when(outside_lo)
-    def _():
-        greet(lower)
-
-    @pl.when(outside_hi)
-    def _():
-        greet(upper)
+    below, beyond = base > 0, base + 4 < n
+    middle = (q == 1) | (q == 2)
+    greet(base + jnp.where(middle, 3 - q, 1 + q // 3))
+
+    @pl.when(middle)
+    def _():
+        greet(base + jnp.where(q == 1, 3, 0))
+
+    @pl.when((h == s) & jnp.where(h == 0, below, beyond))
+    def _():
+        greet(me - 3 + 6 * h)
+
+    @pl.when(middle & jnp.where(h == 0, beyond, below))
+    def _():
+        greet(me + 4 - 8 * h)
 
     zero_rows = jnp.zeros((PAD, nx), jnp.float32)
     outer = pl.multiple_of(h * (PAD + half), PAD)
     inner = pl.multiple_of((1 - h) * (PAD + half), PAD)
 
-    crossing = outside_lo | outside_hi
-
-    @pl.when(crossing)
-    def _():
-        pl.semaphore_wait(barrier, 4)
-
-    @pl.when(jnp.logical_not(crossing))
-    def _():
-        pl.semaphore_wait(barrier, 3)
+    for central in (False, True):
+        for sides in range(3 if central else 1):
+            count = below.astype(jnp.int32) + beyond.astype(jnp.int32)
+
+            @pl.when(middle & (count == sides) if central else jnp.logical_not(middle))
+            def _():
+                pl.semaphore_wait(barrier, 2 + sides if central else 1)
 
     def place(side_half, j):
         return j if side_half == 1 else CHUNKS - 1 - j
@@ -350,16 +352,16 @@
             feed(2, late)
             feed(3, late)
 
-        for which, source, target, begin in ((0, gacc, grad_out, CHUNKS - 2), (1, aacc, adj_out, CHUNKS - 1)):
-            m, final = t - begin, CHUNKS // 2 - 1
-
-            @pl.when((m >= 0) & (m < final))
-            def _():
-                ship(which, source, target, m)
-
-            @pl.when(m == final + 1)
-            def _():
-                ship(which, source, target, final)
+        for which, source, target in ((0, gacc, grad_out), (1, aacc, adj_out)):
+            early, since = t - SHIP - which, t - exchanges - which
+
+            @pl.when((early >= 0) & (early <= SHIP - exchanges) & (early < CHUNKS // 2))
+            def _():
+                ship(which, source, target, early)
+
+            @pl.when((since % 2 == 0) & (since // 2 > SHIP - exchanges) & (since // 2 < CHUNKS // 2))
+            def _():
+                ship(which, source, target, since // 2)
 
         for r in range(min(rounds, ticks - summed)):
             @pl.when(t == summed + r)

time: 145 us -> 144 us (level)
  no operation moved by 1% of the time
where the time goes in v3:
time: 144 us
  Pallas kernels  143 us (99%)
    pallas_call x1, Pallas kernels, on_device(): pl.pallas_call(functools.partial(kernel, n, rounds, float(n * own * ny *...  141 us

profile of v3, /device:TPU:1, one launch (start us, length us, event | category | flops | bytes accessed | tf_op | source)
XLA Modules:
  0.0 144.1 jit_solution(2548181168084027138)
XLA Ops:
  0.6 140.9 %shard_map.67 = (f32[2,512,512]{2,1,0:T(8,128)S(1)}, f32[2,512,512]{2,1,0:T(8,128)S(1)}, f32[8,128]{1,0:T(8,128)S(1)}) custom-call(f32[2,512,512]{2,1,0:T(8,128)} %coef_hbm.1, f32[2,512,512]{2,1,0:T(8,128)} %init_hbm.1, f32[2,512,512]{2,1,0:T(8,128)} %obs_hbm.1, f32[2,512,512]{2,1,0:T(8,128)} %wgt_hbm.1), custom_call_target="tpu_custom_call" | custom-call | tf_op jit(solution)/shard_map/pallas_call | solution.py:445
  141.6 2.5 %shard_map.68 = (f32[2,512,512]{2,1,0:T(8,128)}, f32[2,512,512]{2,1,0:T(8,128)}, f32[1,1]{1,0:T(1,128)}) custom-call(f32[2,512,512]{2,1,0:T(8,128)S(1)} %get-tuple-element.9.grad, f32[2,512,512]{2,1,0:T(8,128)S(1)} %get-tuple-element.10.adj, f32[8,128]{1,0:T(8,128)S(1)} %get-tuple-element.11.misfit), custom_call_target="tpu_custom_call" | custom-call | tf_op jit(solution)/shard_map/pallas_call | solution.py:470

commit v4 on v3

--- a/solution.py
+++ b/solution.py
@@ -14,6 +14,8 @@
 TILE = 8
 CHUNKS = 16
 RING = 4
+GROUP = 4
+SLOTS = 8
 PIECE = 128
 SHIP = 12
 
@@ -43,30 +45,32 @@
 
     hbm = (init_hbm, coef_hbm, obs_hbm, wgt_hbm)
     held = (None, coef, obs, wgt)
+    barrier = pltpu.get_barrier_semaphore()
+
+    def greet(device):
+        pl.semaphore_signal(barrier, inc=1, device_id=(device,), device_id_type=MESH)
+
+    below, beyond = base > 0, base + 4 < n
+    middle = (q == 1) | (q == 2)
+
+    @pl.when(middle)
+    def _():
+        greet(base + jnp.where(q == 1, 3, 0))
+
+    greet(base + jnp.where(middle, 3 - q, 1 + q // 3))
+
+    @pl.when((h == s) & jnp.where(h == 0, below, beyond))
+    def _():
+        greet(me - 3 + 6 * h)
+
+    @pl.when(middle & jnp.where(h == 0, beyond, below))
+    def _():
+        greet(me + 4 - 8 * h)
+
     for array in range(2):
         src = hbm[array].at[:, pl.ds(pl.multiple_of(half - h * rows, PAD), rows), :]
         pltpu.make_async_copy(src, first.at[array], first_sem).start()
 
-    barrier = pltpu.get_barrier_semaphore()
-
-    def greet(device):
-        pl.semaphore_signal(barrier, inc=1, device_id=(device,), device_id_type=MESH)
-
-    below, beyond = base > 0, base + 4 < n
-    middle = (q == 1) | (q == 2)
-    greet(base + jnp.where(middle, 3 - q, 1 + q // 3))
-
-    @pl.when(middle)
-    def _():
-        greet(base + jnp.where(q == 1, 3, 0))
-
-    @pl.when((h == s) & jnp.where(h == 0, below, beyond))
-    def _():
-        greet(me - 3 + 6 * h)
-
-    @pl.when(middle & jnp.where(h == 0, beyond, below))
-    def _():
-        greet(me + 4 - 8 * h)
 
     zero_rows = jnp.zeros((PAD, nx), jnp.float32)
     outer = pl.multiple_of(h * (PAD + half), PAD)
@@ -94,7 +98,7 @@
             else:
                 src = hbm[array].at[:, pl.ds(pl.multiple_of(to * half + row, PAD), rows), :]
                 dst = held[array].at[slot, pl.ds(pl.multiple_of(row, PAD), rows), :]
-            arrived = in_recv.at[array // 2, j]
+            arrived = in_recv.at[array // 2, j % SLOTS]
             distant = dest != me
             if isinstance(j, int) and j == 0:
                 across_chips = q // 2 != to
@@ -122,7 +126,7 @@
         pltpu.make_async_copy(ref, ref, sem).wait()
 
     def fed(kind, j):
-        await_copy(st.at[pl.ds(0, 2), :, pl.ds(0, rows), :], in_recv.at[kind, j])
+        await_copy(st.at[pl.ds(0, 2), :, pl.ds(0, rows), :], in_recv.at[kind, j % SLOTS])
 
     await_copy(first, first_sem)
     for j in range(3):
@@ -162,7 +166,7 @@
             pltpu.make_async_remote_copy(
                 src_ref=st.at[e, (planes - 1) * (1 - side), padded, :],
                 dst_ref=halo.at[side, e, here, :],
-                send_sem=halo_send.at[side], recv_sem=halo_recv.at[e, j % RING],
+                send_sem=halo_send.at[side], recv_sem=halo_recv.at[e // GROUP, (j + e + 1) % RING],
                 device_id=(device,), device_id_type=MESH,
             ).start()
 
@@ -174,17 +178,15 @@
         def _():
             copy(1, lower)
 
-    def receive(e, at, j):
-        here = pl.ds(at, rows)
-        arrived = halo_recv.at[e, j % RING]
-
-        @pl.when(has_lo & has_hi)
-        def _():
-            await_copy(halo.at[:, e, here, :], arrived)
-
-        @pl.when(jnp.logical_not(has_lo & has_hi))
-        def _():
-            await_copy(halo.at[0, e, here, :], arrived)
+    def receive(group, t):
+        first_stage = group * GROUP
+        count = jnp.minimum(first_stage + GROUP, t) - jnp.maximum(first_stage, t - CHUNKS)
+        arrived = halo_recv.at[group, t % RING]
+        for stages in range(1, GROUP + 1):
+            for sides in (1, 2):
+                @pl.when((count == stages) & ((has_lo & has_hi) == (sides == 2)))
+                def _():
+                    await_copy(halo.at[pl.ds(0, sides), pl.ds(0, stages), pl.ds(0, rows), :], arrived)
 
     def edge_copy(e):
         return pltpu.make_async_remote_copy(
@@ -246,7 +248,6 @@
 
         if e == ITERS - 1:
             fed(1, j)
-        receive(e, at, j)
 
         def tile(t, carry):
             row = pl.multiple_of(at + t * TILE, TILE)
@@ -335,6 +336,8 @@
 
         for e in range(exchanges):
             j = t - 1 - e
+            if e % GROUP == 0:
+                receive(e // GROUP, t)
 
             @pl.when((j >= 0) & (j < CHUNKS))
             def _():
@@ -455,8 +458,8 @@
                 pltpu.VMEM((TILE, nx), jnp.float32),
                 pltpu.VMEM((2 * rounds, 8, 128), jnp.float32),
                 edge, edge,
-                dma((2,)), dma((2, CHUNKS)),
-                dma((2,)), dma((exchanges, RING)),
+                dma((2,)), dma((2, SLOTS)),
+                dma((2,)), dma((exchanges // GROUP, RING)),
                 dma, dma((2,)),
                 dma((2,)), dma,
                 dma, dma((rounds,)),

time: 144 us -> 144 us (level)
  no operation moved by 1% of the time
where the time goes in v4:
time: 144 us
  Pallas kernels  143 us (99%)
    pallas_call x1, Pallas kernels, on_device(): pl.pallas_call(functools.partial(kernel, n, rounds, float(n * own * ny *...  141 us

profile of v4, /device:TPU:1, one launch (start us, length us, event | category | flops | bytes accessed | tf_op | source)
XLA Modules:
  0.0 143.8 jit_solution(2231725083002248460)
XLA Ops:
  0.6 140.6 %shard_map.67 = (f32[2,512,512]{2,1,0:T(8,128)S(1)}, f32[2,512,512]{2,1,0:T(8,128)S(1)}, f32[8,128]{1,0:T(8,128)S(1)}) custom-call(f32[2,512,512]{2,1,0:T(8,128)} %coef_hbm.1, f32[2,512,512]{2,1,0:T(8,128)} %init_hbm.1, f32[2,512,512]{2,1,0:T(8,128)} %obs_hbm.1, f32[2,512,512]{2,1,0:T(8,128)} %wgt_hbm.1), custom_call_target="tpu_custom_call" | custom-call | tf_op jit(solution)/shard_map/pallas_call | solution.py:448
  141.3 2.5 %shard_map.68 = (f32[2,512,512]{2,1,0:T(8,128)}, f32[2,512,512]{2,1,0:T(8,128)}, f32[1,1]{1,0:T(1,128)}) custom-call(f32[2,512,512]{2,1,0:T(8,128)S(1)} %get-tuple-element.9.grad, f32[2,512,512]{2,1,0:T(8,128)S(1)} %get-tuple-element.10.adj, f32[8,128]{1,0:T(8,128)S(1)} %get-tuple-element.11.misfit), custom_call_target="tpu_custom_call" | custom-call | tf_op jit(solution)/shard_map/pallas_call | solution.py:473

commit v5 on v4

--- a/solution.py
+++ b/solution.py
@@ -17,7 +17,8 @@
 GROUP = 4
 SLOTS = 8
 PIECE = 128
-SHIP = 12
+SHIP = 13
+SLOW = 2
 
 
 def kernel(n, rounds, cells, coef_hbm, init_hbm, obs_hbm, wgt_hbm, grad_out, adj_out, misfit_out,
@@ -356,15 +357,21 @@
             feed(3, late)
 
         for which, source, target in ((0, gacc, grad_out), (1, aacc, adj_out)):
-            early, since = t - SHIP - which, t - exchanges - which
-
-            @pl.when((early >= 0) & (early <= SHIP - exchanges) & (early < CHUNKS // 2))
-            def _():
-                ship(which, source, target, early)
-
-            @pl.when((since % 2 == 0) & (since // 2 > SHIP - exchanges) & (since // 2 < CHUNKS // 2))
-            def _():
-                ship(which, source, target, since // 2)
+            slow, m = t - SHIP - which, t - SHIP - SLOW
+            final = CHUNKS // 2 - 1
+
+            @pl.when((slow >= 0) & (slow < 2 * SLOW) & (slow % 2 == 0))
+            def _():
+                ship(which, source, target, slow // 2)
+
+            @pl.when((m >= SLOW) & (m <= final - which))
+            def _():
+                ship(which, source, target, m)
+
+            if which == 1:
+                @pl.when(m == final + 1)
+                def _():
+                    ship(which, source, target, final)
 
         for r in range(min(rounds, ticks - summed)):
             @pl.when(t == summed + r)

time: 144 us -> 144 us (level)
  no operation moved by 1% of the time
where the time goes in v5:
time: 144 us
  Pallas kernels  143 us (99%)
    pallas_call x1, Pallas kernels, on_device(): pl.pallas_call(functools.partial(kernel, n, rounds, float(n * own * ny *...  141 us

profile of v5, /device:TPU:1, one launch (start us, length us, event | category | flops | bytes accessed | tf_op | source)
XLA Modules:
  0.0 143.8 jit_solution(17497900067496106530)
XLA Ops:
  0.6 140.6 %shard_map.67 = (f32[2,512,512]{2,1,0:T(8,128)S(1)}, f32[2,512,512]{2,1,0:T(8,128)S(1)}, f32[8,128]{1,0:T(8,128)S(1)}) custom-call(f32[2,512,512]{2,1,0:T(8,128)} %coef_hbm.1, f32[2,512,512]{2,1,0:T(8,128)} %init_hbm.1, f32[2,512,512]{2,1,0:T(8,128)} %obs_hbm.1, f32[2,512,512]{2,1,0:T(8,128)} %wgt_hbm.1), custom_call_target="tpu_custom_call" | custom-call | tf_op jit(solution)/shard_map/pallas_call | solution.py:455
  141.3 2.5 %shard_map.68 = (f32[2,512,512]{2,1,0:T(8,128)}, f32[2,512,512]{2,1,0:T(8,128)}, f32[1,1]{1,0:T(1,128)}) custom-call(f32[2,512,512]{2,1,0:T(8,128)S(1)} %get-tuple-element.9.grad, f32[2,512,512]{2,1,0:T(8,128)S(1)} %get-tuple-element.10.adj, f32[8,128]{1,0:T(8,128)S(1)} %get-tuple-element.11.misfit), custom_call_target="tpu_custom_call" | custom-call | tf_op jit(solution)/shard_map/pallas_call | solution.py:480

commit v6 on v5

--- a/solution.py
+++ b/solution.py
@@ -43,6 +43,7 @@
         partners.append(me + bit * (1 - 2 * ((me // bit) % 2)))
     sums = [partners[0]] + partners[2:]
     free = s == h
+    ahead = h == 1
 
     hbm = (init_hbm, coef_hbm, obs_hbm, wgt_hbm)
     held = (None, coef, obs, wgt)
@@ -351,7 +352,9 @@
 
         late = t + 2 - ITERS + 1
 
-        @pl.when((late >= 0) & (late < CHUNKS))
+        late = jnp.where(ahead & (t == 0), 0, late)
+
+        @pl.when((late >= 0) & (late < CHUNKS) & jnp.logical_not(ahead & (t == 1)))
         def _():
             feed(2, late)
             feed(3, late)
@@ -390,33 +393,35 @@
     misfit_out[...] = jnp.sqrt(jnp.broadcast_to(whole, (8, 128)) / cells + 1e-06)
 
     slabs = st.at[pl.ds(0, 2), :, pl.ds(0, half), :]
-    await_copy(slabs, out_recv)
+    for to in range(2):
+        @pl.when(base + 2 * to + q // 2 != me)
+        def _():
+            await_copy(slabs, in_send.at[to])
+
+    @pl.when(has_hi)
+    def _():
+        await_copy(halo.at[0], halo_send.at[0])
+
+    @pl.when(has_lo)
+    def _():
+        await_copy(halo.at[1], halo_send.at[1])
+
+    await_copy(edge_out, edge_send)
+
+    @pl.when(free)
+    def _():
+        await_copy(part.at[pl.ds(0, rounds + 1)], psend_sem)
+
+    @pl.when(jnp.logical_not(free))
+    def _():
+        await_copy(part.at[pl.ds(0, rounds - 1)], psend_sem)
+
     for o in range(2):
         @pl.when(base + 2 * s + o != me)
         def _():
             await_copy(coef, out_send.at[o])
-    for to in range(2):
-        @pl.when(base + 2 * to + q // 2 != me)
-        def _():
-            await_copy(slabs, in_send.at[to])
-
-    @pl.when(has_hi)
-    def _():
-        await_copy(halo.at[0], halo_send.at[0])
-
-    @pl.when(has_lo)
-    def _():
-        await_copy(halo.at[1], halo_send.at[1])
-
-    await_copy(edge_out, edge_send)
-
-    @pl.when(free)
-    def _():
-        await_copy(part.at[pl.ds(0, rounds + 1)], psend_sem)
-
-    @pl.when(jnp.logical_not(free))
-    def _():
-        await_copy(part.at[pl.ds(0, rounds - 1)], psend_sem)
+
+    await_copy(slabs, out_recv)
 
 
 def finish(grad, adj, misfit, grad_out, adj_out, misfit_out, scaled, sem):

time: 144 us -> 144 us (level)
  no operation moved by 1% of the time
where the time goes in v6:
time: 144 us
  Pallas kernels  143 us (99%)
    pallas_call x1, Pallas kernels, on_device(): pl.pallas_call(functools.partial(kernel, n, rounds, float(n * own * ny *...  141 us

profile of v6, /device:TPU:1, one launch (start us, length us, event | category | flops | bytes accessed | tf_op | source)
XLA Modules:
  0.0 143.8 jit_solution(17481403108588920762)
XLA Ops:
  0.6 140.6 %shard_map.67 = (f32[2,512,512]{2,1,0:T(8,128)S(1)}, f32[2,512,512]{2,1,0:T(8,128)S(1)}, f32[8,128]{1,0:T(8,128)S(1)}) custom-call(f32[2,512,512]{2,1,0:T(8,128)} %coef_hbm.1, f32[2,512,512]{2,1,0:T(8,128)} %init_hbm.1, f32[2,512,512]{2,1,0:T(8,128)} %obs_hbm.1, f32[2,512,512]{2,1,0:T(8,128)} %wgt_hbm.1), custom_call_target="tpu_custom_call" | custom-call | tf_op jit(solution)/shard_map/pallas_call | solution.py:460
  141.2 2.5 %shard_map.68 = (f32[2,512,512]{2,1,0:T(8,128)}, f32[2,512,512]{2,1,0:T(8,128)}, f32[1,1]{1,0:T(1,128)}) custom-call(f32[2,512,512]{2,1,0:T(8,128)S(1)} %get-tuple-element.9.grad, f32[2,512,512]{2,1,0:T(8,128)S(1)} %get-tuple-element.10.adj, f32[8,128]{1,0:T(8,128)S(1)} %get-tuple-element.11.misfit), custom_call_target="tpu_custom_call" | custom-call | tf_op jit(solution)/shard_map/pallas_call | solution.py:485

commit v7 on v6

--- a/solution.py
+++ b/solution.py
@@ -16,7 +16,7 @@
 RING = 4
 GROUP = 4
 SLOTS = 8
-PIECE = 128
+PIECE = 64
 SHIP = 13
 SLOW = 2
 

time: 144 us -> 144 us (level)
  no operation moved by 1% of the time
where the time goes in v7:
time: 144 us
  Pallas kernels  143 us (99%)
    pallas_call x1, Pallas kernels, on_device(): pl.pallas_call(functools.partial(kernel, n, rounds, float(n * own * ny *...  141 us

profile of v7, /device:TPU:1, one launch (start us, length us, event | category | flops | bytes accessed | tf_op | source)
XLA Modules:
  0.0 143.8 jit_solution(8192374128013653723)
XLA Ops:
  0.6 140.6 %shard_map.67 = (f32[2,512,512]{2,1,0:T(8,128)S(1)}, f32[2,512,512]{2,1,0:T(8,128)S(1)}, f32[8,128]{1,0:T(8,128)S(1)}) custom-call(f32[2,512,512]{2,1,0:T(8,128)} %coef_hbm.1, f32[2,512,512]{2,1,0:T(8,128)} %init_hbm.1, f32[2,512,512]{2,1,0:T(8,128)} %obs_hbm.1, f32[2,512,512]{2,1,0:T(8,128)} %wgt_hbm.1), custom_call_target="tpu_custom_call" | custom-call | tf_op jit(solution)/shard_map/pallas_call | solution.py:460
  141.2 2.5 %shard_map.68 = (f32[2,512,512]{2,1,0:T(8,128)}, f32[2,512,512]{2,1,0:T(8,128)}, f32[1,1]{1,0:T(1,128)}) custom-call(f32[2,512,512]{2,1,0:T(8,128)S(1)} %get-tuple-element.9.grad, f32[2,512,512]{2,1,0:T(8,128)S(1)} %get-tuple-element.10.adj, f32[8,128]{1,0:T(8,128)S(1)} %get-tuple-element.11.misfit), custom_call_target="tpu_custom_call" | custom-call | tf_op jit(solution)/shard_map/pallas_call | solution.py:485
